TPU v7x, 256 devices: a whole 4x4x8 slice. The times are simulated.
256 devices in a mesh: dp: 32 (over x, y, core), tensor: 8 (over z).
Axes of the slice: x: 4, y: 4, z: 8, core: 2. Of those that a mesh axis runs over, the one named last changes fastest.
Arguments:
- proxy_hidden: bfloat16 [1536, 4096], P('dp', 'tensor'), may hold values from -176.625 to 176.625
- reference_hidden: bfloat16 [1536, 4096], P('dp', 'tensor'), may hold values from -176.625 to 176.625
- proxy_head: bfloat16 [128256, 4096], P(('dp', 'tensor')), may hold values from -0.09375 to 0.09375
- reference_head: bfloat16 [128256, 4096], P(('dp', 'tensor')), may hold values from -0.09375 to 0.09375
- targets: int32 [1536], P('dp'), may hold values from 0 to 128255
- domains: int32 [1536], P('dp'), may hold values from 0 to 127
- keep_mask: int32 [1536], P('dp'), may hold values 0 or 1
- prior_weights: float32 [128], replicated, may hold values from 0.5 to 2
Outputs:
- excess: float32 [1536], P('dp')
- log_weights: float32 [128], replicated
All inputs are finite; a program needn't handle non-finite values. No bound on the sum of `keep_mask` on one device may be relied on, other than what follows from the above.
Results may differ from a plain program's by a relative error of at most 0.00045.
Values may be sent and summed in bfloat16 or wider, within the bound.
A program may use at most 128 MiB of HBM per device.

v0:
```python
import jax
import jax.numpy as jnp
from jax import lax
from jax.sharding import Mesh
from jax.sharding import PartitionSpec as P

DOMAINS = 128
STEPS = 3
DP = ("dp_0", "dp_1", "dp_2")
DP_TENSOR = ("dp_0", "dp_1", "dp_2", "tensor")
step_size = 1.0
smoothing = 0.001


def gather_turned(arrays, axis, dims):
    turned = [jnp.moveaxis(a, dim, 0) for a, dim in zip(arrays, dims)]
    widths = [t[0].size for t in turned]
    both = jnp.concatenate([t.reshape(-1, w) for t, w in zip(turned, widths)], axis=1)
    whole = lax.all_gather(both, axis, axis=0, tiled=True)
    pieces = jnp.split(whole, [sum(widths[:k]) for k in range(1, len(widths))], axis=1)
    return tuple(
        (
            jnp.moveaxis(b.reshape(-1, *t.shape[1:]), 0, dim)
            for b, t, dim in zip(pieces, turned, dims)
        )
    )


def copy_for_each(array, axis):
    copies = jnp.broadcast_to(array, (lax.axis_size(axis), *array.shape))
    return lax.all_to_all(copies, axis, split_axis=0, concat_axis=0, tiled=True)


def in_order(pieces, dim):
    dims = list(pieces.shape[1:])
    dims[dim] *= pieces.shape[0]
    return jnp.moveaxis(pieces, 0, dim).reshape(dims)


def gather_directly(array, axis, dim):
    pieces = copy_for_each(array, axis)
    return in_order(pieces, dim)


def all_in_one(array, axis):
    leaves = jax.tree.leaves(array)
    turns = sorted(range(len(leaves)), key=lambda k: -leaves[k].size)
    width = (1, *leaves[turns[0]].shape)[-1]
    lines = [
        jnp.pad(leaves[k].reshape(-1), (0, -leaves[k].size % width)).reshape(-1, width)
        for k in turns
    ]
    both, at, found = (lax.all_gather(jnp.concatenate(lines), axis), 0, {})
    for k, line in zip(turns, lines):
        share = both[:, at : at + len(line)].reshape(len(both), -1)
        found[k] = share[:, : leaves[k].size].reshape(-1, *leaves[k].shape)
        at += len(line)
    numbers = iter(range(len(leaves)))
    return jax.tree.map(lambda _: found[next(numbers)], array)


def combined_by_axis(array, axes, combine):
    for axis in axes:
        pieces = all_in_one(array, axis)
        array = jax.tree.map(lambda part: part[0], pieces)
        for k in range(1, lax.axis_size(axis)):
            array = combine(array, jax.tree.map(lambda part: part[k], pieces))
    return array


def project(rows, head):
    return lax.dot_general(rows, head, (((1,), (1,)), ((), ())), preferred_element_type=jnp.float32)


def row_stats(logits, wanted):
    columns = jnp.arange(logits.shape[1], dtype=jnp.int32)
    row_peak = jnp.max(logits, axis=1)
    row_total = jnp.sum(jnp.exp(logits - row_peak[:, None]), axis=1)
    matched = wanted[:, None] == columns[None, :]
    row_hit = jnp.sum(jnp.where(matched, logits, 0.0), axis=1)
    return jnp.stack([row_peak, row_total, row_hit])


def update_weights(prior_weights, clipped, domains, keep):
    weights = prior_weights / jnp.sum(prior_weights)
    batch_rows = clipped.shape[0] // STEPS
    labels = jnp.arange(DOMAINS, dtype=jnp.int32)
    for section_index in range(STEPS):
        row_start = section_index * batch_rows
        block_loss = clipped[row_start : row_start + batch_rows]
        block_keep = keep[row_start : row_start + batch_rows]
        member = (domains[row_start : row_start + batch_rows][:, None] == labels[None, :]).astype(
            jnp.float32
        )
        domain_sum = jnp.dot(block_loss, member, precision=lax.Precision.HIGHEST)
        domain_count = jnp.dot(block_keep, member, precision=lax.Precision.HIGHEST)
        domain_gain = domain_sum / jnp.maximum(domain_count, 1.0)
        raised = weights * jnp.exp(step_size * domain_gain)
        weights = (1.0 - smoothing) * raised / jnp.sum(raised) + smoothing / DOMAINS
    return jnp.log(weights)


def merge_stats(earlier_part, second_part):
    peak_one, total_one, hit_one = earlier_part
    peak_two, total_two, hit_two = second_part
    top_value = jnp.maximum(peak_one, peak_two)
    joined = total_one * jnp.exp(peak_one - top_value) + total_two * jnp.exp(peak_two - top_value)
    return (top_value, joined, hit_one + hit_two)


def local(
    proxy_hidden,
    reference_hidden,
    proxy_head,
    reference_head,
    targets,
    domains,
    keep_mask,
    prior_weights,
):
    all_targets, all_domains, all_keep = gather_turned((targets, domains, keep_mask), DP, (0, 0, 0))
    vocab_dev = proxy_head.shape[0]
    offset = (lax.axis_index(DP) * lax.axis_size("tensor") + lax.axis_index("tensor")) * vocab_dev
    local_target = all_targets - offset
    stacked = jnp.stack([proxy_hidden, reference_hidden])
    full_rows = gather_directly(stacked, "tensor", 2)
    portion = lax.all_gather(full_rows, DP, axis=1, tiled=True)
    proxy_part = row_stats(project(portion[0], proxy_head), local_target)
    reference_part = row_stats(project(portion[1], reference_head), local_target)
    stats = jnp.concatenate([proxy_part, reference_part], axis=0)
    local_peaks = jnp.stack([stats[0], stats[3]])
    local_totals = jnp.stack([stats[1], stats[4]])
    local_hits = jnp.stack([stats[2], stats[5]])
    global_peak, totals, hit_sum = combined_by_axis(
        (local_peaks, local_totals, local_hits), DP_TENSOR, merge_stats
    )
    losses = global_peak + jnp.log(totals) - hit_sum
    keep = all_keep.astype(jnp.float32)
    loss_gap = losses[0] - losses[1]
    excess_all = loss_gap * keep
    clipped = jnp.maximum(loss_gap, 0.0) * keep
    log_weights = update_weights(prior_weights, clipped, all_domains, keep)
    tok_dev = targets.shape[0]
    mine = lax.dynamic_slice_in_dim(excess_all, lax.axis_index(DP) * tok_dev, tok_dev, 0)
    return (mine, log_weights)


def solution(mesh):
    split = Mesh(
        mesh.devices.reshape(4, 4, 2, mesh.shape["tensor"]), ("dp_0", "dp_1", "dp_2", "tensor")
    )
    return jax.shard_map(
        local,
        mesh=split,
        in_specs=(
            P(DP, "tensor"),
            P(DP, "tensor"),
            P(DP_TENSOR, None),
            P(DP_TENSOR, None),
            P(DP),
            P(DP),
            P(DP),
            P(),
        ),
        out_specs=(P(DP), P()),
        check_vma=False,
    )
```

profile of v0, /device:TPU:2, one launch (start us, length us, event | category | flops | bytes accessed | tf_op | source)
XLA Modules:
  0.0 223.1 jit_solution(5851774989392335685)
XLA Ops:
  7.3 0.8 pad_maximum_fusion
  8.2 31.4 %all_to_all.5 = bf16[8,2,48,512]{3,2,1,0:T(8,128)(2,1)S(1)} all-to-all(bf16[8,2,48,512]{3,2,1,0:T(8,128)(2,1)S(1)} %broadcast_in_dim.7), channel_id=1, replica_groups=mesh['dp_0'=4,'dp_1'=4,'dp_2'=2,'tensor'=8] {'tensor'}, dimensions={0} | all-to-all | bytes 1572864 | tf_op jit(solution)/shard_map/all_to_all | solution.py:31
  39.5 1.0 copy.13
  40.6 24.7 %all-gather.4 = s32[32,48,3]{1,2,0:T(4,128)S(1)} all-gather(s32[1,48,3]{1,2,0:T(4,128)S(1)} %add_bitcast_fusion), channel_id=1, replica_groups=mesh['dp_0'=4,'dp_1'=4,'dp_2'=2,'tensor'=8] {'dp_0','dp_1','dp_2'}, dimensions={0}, use_global_device_ids=true | all-gather | bytes 19008 | tf_op jit(solution)/shard_map/all_gather | solution.py:19
  65.3 0.1 reshape.79
  65.5 0.6 reduce_sum.76
  66.1 0.3 fusion.9
  66.4 0.3 fusion.5
  66.7 0.3 fusion.13
  67.0 67.0 %all-gather.11.cloned.1.call-done = bf16[2,1536,4096]{2,1,0:T(8,128)(2,1)} async-done(((bf16[2,48,4096]{2,1,0:T(8,128)(2,1)}), bf16[2,1536,4096]{2,1,0:T(8,128)(2,1)}) %all-gather.11.cloned.1.call-update) | async-done | bytes 25165840 | tf_op jit(solution)/shard_map/all_gather | solution.py:127
  134.0 10.6 %fusion.94 = (f32[1536]{0:T(1024)S(1)}, f32[1536,501]{0,1:T(8,128)S(1)}) fusion(bf16[501,4096]{1,0:T(8,128)(2,1)} %param.10, bf16[2,1536,4096]{2,1,0:T(8,128)(2,1)} %all-gather.11.cloned.1.call-done), kind=kOutput, calls=%fused_computation.175 | convolution fusion | flops 6304806912 | bytes 19795968 | tf_op jit(solution)/shard_map/dot_general | solution.py:72
  144.7 9.7 %fusion.95 = (f32[1536]{0:T(1024)S(1)}, f32[1536,501]{0,1:T(8,128)S(1)}) fusion(bf16[501,4096]{1,0:T(8,128)(2,1)S(1)} %copy-done.3, bf16[2,1536,4096]{2,1,0:T(8,128)(2,1)} %all-gather.11.cloned.1.call-done), kind=kOutput, calls=%fused_computation.176 | convolution fusion | flops 6304806912 | bytes 19771392 | tf_op jit(solution)/shard_map/dot_general | solution.py:72
  154.4 1.5 select_reduce_fusion
  156.0 12.4 %all-gather.5 = f32[4,6,1536]{2,1,0:T(8,128)S(1)} all-gather(f32[1,6,1536]{2,1,0:T(8,128)S(1)} %bitcast.371), channel_id=2, replica_groups=mesh['dp_0'=4,'dp_1'=4,'dp_2'=2,'tensor'=8] {'dp_0'}, dimensions={0}, use_global_device_ids=true | all-gather | bytes 184320 | tf_op jit(solution)/shard_map/all_gather | solution.py:53
  168.4 0.1 fusion.61
  168.5 12.1 %all-gather.6 = f32[4,6,1536]{2,1,0:T(8,128)S(1)} all-gather(f32[1,6,1536]{2,1,0:T(8,128)S(1)} %maximum_bitcast_fusion), channel_id=3, replica_groups=mesh['dp_0'=4,'dp_1'=4,'dp_2'=2,'tensor'=8] {'dp_1'}, dimensions={0}, use_global_device_ids=true | all-gather | bytes 184320 | tf_op jit(solution)/shard_map/all_gather | solution.py:53
  180.8 1.9 all-gather.7
  182.7 26.7 %all-gather.8 = f32[8,6,1536]{2,1,0:T(8,128)S(1)} all-gather(f32[1,6,1536]{2,1,0:T(8,128)S(1)} %maximum_bitcast_fusion.2), channel_id=5, replica_groups=mesh['dp_0'=4,'dp_1'=4,'dp_2'=2,'tensor'=8] {'tensor'}, dimensions={0}, use_global_device_ids=true | all-gather | bytes 331776 | tf_op jit(solution)/shard_map/all_gather | solution.py:53
  209.4 0.2 fusion.21
  209.7 0.6 dynamic-slice_multiply_fusion
  210.3 1.6 fusion.96
  211.9 1.6 fusion.97
  213.5 1.6 fusion.98
  215.1 1.2 add_log_fusion
  (36 shorter events, 0.6 us)
Async XLA Ops:
  7.2 33.4 %copy-start = (s32[48]{0:T(128)S(1)}, s32[48]{0:T(128)}, u32[]{:S(2)}) copy-start(s32[48]{0:T(128)} %param.14) | copy-start | bytes 580
  7.2 33.4 %copy-start.1 = (s32[48]{0:T(128)S(1)}, s32[48]{0:T(128)}, u32[]{:S(2)}) copy-start(s32[48]{0:T(128)} %param.13) | copy-start | bytes 580
  7.2 33.4 %copy-start.2 = (s32[48]{0:T(128)S(1)}, s32[48]{0:T(128)}, u32[]{:S(2)}) copy-start(s32[48]{0:T(128)} %param.12) | copy-start | bytes 580
  7.2 58.3 %copy-start.4 = (f32[128]{0:T(128)S(1)}, f32[128]{0:T(128)}, u32[]{:S(2)}) copy-start(f32[128]{0:T(128)} %param.15) | copy-start | bytes 1540
  7.2 126.8 %all-gather.11.cloned.1.call-start = ((), (), s32[]{:S(2)}) async-start(), calls=%async_computation.1 | async-start | bytes 25952256 | tf_op jit(solution)/shard_map/all_gather | solution.py:127
  134.0 10.7 %copy-start.3 = (bf16[501,4096]{1,0:T(8,128)(2,1)S(1)}, bf16[501,4096]{1,0:T(8,128)(2,1)}, u32[]{:S(2)}) copy-start(bf16[501,4096]{1,0:T(8,128)(2,1)} %param.11) | copy-start | bytes 12312580
Sparse Core Ops, SparseCore 0:
  40.7 93.2 all-gather.10
where the time goes:
time: 223 us
  blocking collectives  109 us (49%)
  waiting for transfers between devices  67 us (30%)
  matrix products  26 us (12%)
  between operations  14.3 us (6%)
  other arithmetic  5.31 us (2%)
    all_gather x1, waiting for transfers between devices, local(): portion = lax.all_gather(full_rows, DP, axis=1, tiled=True)  67 us
    all_gather x4, blocking collectives, all_in_one(): both, at, found = (lax.all_gather(jnp.concatenate(lines), axis), 0, {})  53.1 us
    all_to_all x1, blocking collectives, copy_for_each(): return lax.all_to_all(copies, axis, split_axis=0, concat_axis=0, tiled=True)  31.4 us
    all_gather x1, blocking collectives, gather_turned(): whole = lax.all_gather(both, axis, axis=0, tiled=True)  24.7 us
    dot_general x2, matrix products, project(): lax.dot_general(rows, head, (((1,), (1,)), ((), ())), preferred_element_t...  20.3 us
    dot_general x3, matrix products, update_weights(): domain_sum = jnp.dot(block_loss, member, precision=lax.Precision.HIGHEST)  4.82 us
  transfers between devices with their start and end apart: 1, of which 1 were waited for; matrix products, arithmetic and copies ran while one was open for 1% of the time, Pallas kernels for 0%

commit v1 on v0

--- a/solution.py
+++ b/solution.py
@@ -124,7 +124,9 @@
     local_target = all_targets - offset
     stacked = jnp.stack([proxy_hidden, reference_hidden])
     full_rows = gather_directly(stacked, "tensor", 2)
-    portion = lax.all_gather(full_rows, DP, axis=1, tiled=True)
+    portion = jnp.concatenate(
+        lax.all_to_all(jnp.stack([full_rows] * lax.axis_size(DP)), DP, 0, 0), axis=1
+    )
     proxy_part = row_stats(project(portion[0], proxy_head), local_target)
     reference_part = row_stats(project(portion[1], reference_head), local_target)
     stats = jnp.concatenate([proxy_part, reference_part], axis=0)

time: 223 us -> 565 us (2.53)
  blocking collectives: 109 us -> 508 us
  waiting for transfers between devices: 67 us -> 0.01 us
  local copies, waits for them, and re-layouts: 1.33 us -> 19.2 us
  between operations: 14.3 us -> 0.91 us
  starting transfers between devices: 0.04 us -> 7.82 us
    all_gather x1, blocking collectives: 24.7 us -> 427 us  [gather_turned(): whole = lax.all_gather(both, axis, axis=0, tiled=True)]
    all_gather x1 -> x0, waiting for transfers between devices: 67 us -> none  [local(): portion = lax.all_gather(full_rows, DP, axis=1, tiled=True)]
    slice x0 -> x1, local copies, waits for them, and re-layouts: none -> 10.2 us  [local(): portion[1]]
    another operation x0 -> x2, local copies, waits for them, and re-layouts: none -> 8.64 us  [local(): jnp.stack([full_rows] * lax.axis_size(DP))]
    all_to_all x0 -> x1, starting transfers between devices: none -> 7.82 us  [local(): lax.all_to_all(jnp.stack([full_rows] * lax.axis_size(DP)), DP, 0, 0)]
  transfers between devices with their start and end apart: 1 -> 1, of which waited for: 1 -> 0; matrix products, arithmetic and copies ran while one was open for 1% -> 0% of each run, Pallas kernels for 0% -> 0%
where the time goes in v1:
time: 565 us
  blocking collectives  508 us (90%)
  matrix products  23.4 us (4%)
  local copies, waits for them, and re-layouts  19.2 us (3%)
  starting transfers between devices  7.82 us (1%)
    all_gather x1, blocking collectives, gather_turned(): whole = lax.all_gather(both, axis, axis=0, tiled=True)  427 us
    all_gather x4, blocking collectives, all_in_one(): both, at, found = (lax.all_gather(jnp.concatenate(lines), axis), 0, {})  50 us
    all_to_all x1, blocking collectives, copy_for_each(): return lax.all_to_all(copies, axis, split_axis=0, concat_axis=0, tiled=True)  31.4 us
    dot_general x2, matrix products, project(): lax.dot_general(rows, head, (((1,), (1,)), ((), ())), preferred_element_t...  17.8 us
  transfers between devices with their start and end apart: 1, of which 0 were waited for; matrix products, arithmetic and copies ran while one was open for 0% of the time, Pallas kernels for 0%

profile of v1, /device:TPU:2, one launch (start us, length us, event | category | flops | bytes accessed | tf_op | source)
XLA Modules:
  0.0 565.0 jit_solution(10726857088745858741)
XLA Ops:
  0.6 0.8 pad_maximum_fusion
  1.5 31.4 %all_to_all.10 = bf16[8,2,48,512]{3,2,1,0:T(8,128)(2,1)S(1)} all-to-all(bf16[8,2,48,512]{3,2,1,0:T(8,128)(2,1)S(1)} %broadcast_in_dim.7), channel_id=1, replica_groups=mesh['dp_0'=4,'dp_1'=4,'dp_2'=2,'tensor'=8] {'tensor'}, dimensions={0} | all-to-all | bytes 1572864 | tf_op jit(solution)/shard_map/all_to_all | solution.py:31
  33.0 8.6 %stack.36 = bf16[32,2,48,4096]{3,2,1,0:T(8,128)(2,1)} broadcast(bf16[2,48,4096]{2,1,0:T(8,128)(2,1)S(1)} %bitcast.366), dimensions={1,2,3} | broadcast | bytes 25952256 | tf_op jit(solution)/shard_map/stack | solution.py:128
  41.6 7.8 %all-to-all-start.1 = ((bf16[32,2,48,4096]{3,2,1,0:T(8,128)(2,1)}), bf16[32,2,48,4096]{3,2,1,0:T(8,128)(2,1)}, u32[]{:S(2)}, u32[]{:S(2)}) async-start(bf16[32,2,48,4096]{3,2,1,0:T(8,128)(2,1)} %stack.36), calls=%async_computation.1 | async-start | bytes 50331648 | tf_op jit(solution)/shard_map/all_to_all | solution.py:128
  49.5 426.9 %all-gather.4 = s32[32,48,3]{1,2,0:T(4,128)S(1)} all-gather(s32[1,48,3]{1,2,0:T(4,128)S(1)} %add_bitcast_fusion), channel_id=1, replica_groups=mesh['dp_0'=4,'dp_1'=4,'dp_2'=2,'tensor'=8] {'dp_0','dp_1','dp_2'}, dimensions={0}, use_global_device_ids=true | all-gather | bytes 19008 | tf_op jit(solution)/shard_map/all_gather | solution.py:19
  476.4 0.1 reshape.86
  476.5 0.6 reduce_sum.76
  477.2 0.3 fusion.7
  477.5 0.3 fusion.3
  477.8 0.3 fusion.11
  478.1 10.2 %fusion.90 = (bf16[1,32,48,4096]{3,2,0,1:T(8,128)(2,1)S(1)}, bf16[1,32,48,4096]{3,2,0,1:T(8,128)(2,1)S(1)}) fusion(bf16[2,32,48,4096]{3,2,0,1:T(8,128)(2,1)} %bitcast.3), kind=kLoop, calls=%fused_computation.169 | loop fusion | bytes 50331648 | tf_op jit(solution)/shard_map/slice | solution.py:131
  488.3 8.9 %fusion.93 = (f32[1536]{0:T(1024)S(1)}, f32[1536,501]{0,1:T(8,128)S(1)}) fusion(bf16[1536,4096]{1,0:T(8,128)(2,1)S(1)} %bitcast.365, bf16[501,4096]{1,0:T(8,128)(2,1)} %param.10), kind=kOutput, calls=%fused_computation.172 | convolution fusion | flops 6304806912 | bytes 19771392 | tf_op jit(solution)/shard_map/dot_general | solution.py:72
  497.2 8.9 %fusion.94 = (f32[1536]{0:T(1024)S(1)}, f32[1536,501]{0,1:T(8,128)S(1)}) fusion(bf16[1536,4096]{1,0:T(8,128)(2,1)S(1)} %bitcast.364, bf16[501,4096]{1,0:T(8,128)(2,1)} %param.11), kind=kOutput, calls=%fused_computation.173 | convolution fusion | flops 6304806912 | bytes 19771392 | tf_op jit(solution)/shard_map/dot_general | solution.py:72
  506.1 1.5 select_reduce_fusion
  507.7 11.0 %all-gather.5 = f32[4,6,1536]{2,1,0:T(8,128)S(1)} all-gather(f32[1,6,1536]{2,1,0:T(8,128)S(1)} %bitcast.368), channel_id=2, replica_groups=mesh['dp_0'=4,'dp_1'=4,'dp_2'=2,'tensor'=8] {'dp_0'}, dimensions={0}, use_global_device_ids=true | all-gather | bytes 184320 | tf_op jit(solution)/shard_map/all_gather | solution.py:53
  518.9 12.1 %all-gather.6 = f32[4,6,1536]{2,1,0:T(8,128)S(1)} all-gather(f32[1,6,1536]{2,1,0:T(8,128)S(1)} %maximum_bitcast_fusion), channel_id=3, replica_groups=mesh['dp_0'=4,'dp_1'=4,'dp_2'=2,'tensor'=8] {'dp_1'}, dimensions={0}, use_global_device_ids=true | all-gather | bytes 184320 | tf_op jit(solution)/shard_map/all_gather | solution.py:53
  531.1 1.9 all-gather.7
  533.1 25.0 %all-gather.8 = f32[8,6,1536]{2,1,0:T(8,128)S(1)} all-gather(f32[1,6,1536]{2,1,0:T(8,128)S(1)} %maximum_bitcast_fusion.2), channel_id=5, replica_groups=mesh['dp_0'=4,'dp_1'=4,'dp_2'=2,'tensor'=8] {'tensor'}, dimensions={0}, use_global_device_ids=true | all-gather | bytes 331776 | tf_op jit(solution)/shard_map/all_gather | solution.py:53
  558.1 0.2 fusion.19
  558.4 0.6 dynamic-slice_multiply_fusion
  559.0 1.6 fusion.95
  560.6 1.6 fusion.96
  562.2 1.6 fusion.97
  563.8 1.2 add_log_fusion
  (35 shorter events, 0.7 us)
Async XLA Ops:
  41.6 7.8 %copy-start = (s32[48]{0:T(128)S(1)}, s32[48]{0:T(128)}, u32[]{:S(2)}) copy-start(s32[48]{0:T(128)} %param.14) | copy-start | bytes 580
  41.6 7.9 %copy-start.1 = (s32[48]{0:T(128)S(1)}, s32[48]{0:T(128)}, u32[]{:S(2)}) copy-start(s32[48]{0:T(128)} %param.13) | copy-start | bytes 580
  41.6 7.9 %copy-start.2 = (s32[48]{0:T(128)S(1)}, s32[48]{0:T(128)}, u32[]{:S(2)}) copy-start(s32[48]{0:T(128)} %param.12) | copy-start | bytes 580
  41.6 434.9 %copy-start.3 = (f32[128]{0:T(128)S(1)}, f32[128]{0:T(128)}, u32[]{:S(2)}) copy-start(f32[128]{0:T(128)} %param.15) | copy-start | bytes 1540
  41.6 436.5 %all-to-all-start.1 = ((bf16[32,2,48,4096]{3,2,1,0:T(8,128)(2,1)}), bf16[32,2,48,4096]{3,2,1,0:T(8,128)(2,1)}, u32[]{:S(2)}, u32[]{:S(2)}) async-start(bf16[32,2,48,4096]{3,2,1,0:T(8,128)(2,1)} %stack.36), calls=%async_computation.1 | async-start | bytes 50331648 | tf_op jit(solution)/shard_map/all_to_all | solution.py:128
